TPU v7x, 32 devices: a whole 2x2x4 slice. The times are simulated.
32 devices in a mesh: rep: 8 (over z, y), fsdp: 4 (over x, core).
Axes of the slice: x: 2, y: 2, z: 4, core: 2. Of those that a mesh axis runs over, the one named last changes fastest.
Arguments:
- gradients: bfloat16 [8, 4, 1024, 2048], P('rep', 'fsdp'), may hold values from -6 to 6
- momentum: float32 [8, 1024, 2048], P('rep', None, 'fsdp'), may hold values from -12 to 12
- master_weights: float32 [1024, 2048], P(None, 'fsdp'), may hold values from -0.125 to 0.125
Outputs:
- new_momentum: float32 [8, 1024, 2048], P('rep', None, 'fsdp')
- new_master: float32 [1024, 2048], P(None, 'fsdp')
- weights_full: bfloat16 [1024, 2048], replicated
All inputs are finite; a program needn't handle non-finite values.
Results may differ from a plain program's by a relative error of at most 0.012.
Values may be sent and summed in bfloat16 or wider, within the bound.
A program may use at most 128 MiB of HBM per device.

v0:
```python
import jax
import jax.numpy as jnp
from jax import lax
from jax.sharding import PartitionSpec as P

GROUP = 128
BAND = 16
momentum_decay = 0.9
step_size = 0.05


def cosine_rows():
    freq = jnp.arange(BAND, dtype=jnp.float32)[:, None]
    place = jnp.arange(GROUP, dtype=jnp.float32)[None, :]
    factor = jnp.where(freq == 0.0, jnp.sqrt(1.0 / GROUP), jnp.sqrt(2.0 / GROUP)).astype(
        jnp.float32
    )
    return factor * jnp.cos(jnp.pi * (2.0 * place + 1.0) * freq / (2.0 * GROUP))


def band_of(matrix):
    table = cosine_rows()
    blocks = matrix.reshape(matrix.shape[0] // GROUP, GROUP, matrix.shape[1] // GROUP, GROUP)
    return jnp.einsum("kr,arbc,lc->abkl", table, blocks, table, precision=lax.Precision.HIGHEST)


def spread_band(coeffs):
    table = cosine_rows()
    blocks = jnp.einsum("kr,abkl,lc->arbc", table, coeffs, table, precision=lax.Precision.HIGHEST)
    return blocks.reshape(coeffs.shape[0] * GROUP, coeffs.shape[1] * GROUP)


def local(gradients, momentum, master_weights):
    summed = lax.psum_scatter(
        gradients[0, 0].astype(jnp.float32).astype(jnp.bfloat16),
        "fsdp",
        scatter_dimension=1,
        tiled=True,
    ).astype(jnp.float32)
    moment = momentum_decay * momentum[0] + summed
    own_band = band_of(moment)
    remaining = moment - spread_band(own_band)
    mean_band = lax.psum(own_band, "rep") / lax.axis_size("rep")
    new_master = master_weights - step_size * spread_band(mean_band)
    weights_full = lax.all_gather(new_master.astype(jnp.bfloat16), "fsdp", axis=1, tiled=True)
    return (remaining[None], new_master, weights_full)


def solution(mesh):
    return jax.shard_map(
        local,
        mesh=mesh,
        in_specs=(P("rep", "fsdp", None, None), P("rep", None, "fsdp"), P(None, "fsdp")),
        out_specs=(P("rep", None, "fsdp"), P(None, "fsdp"), P()),
        check_vma=False,
    )
```

profile of v0, /device:TPU:0, one launch (start us, length us, event | category | flops | bytes accessed | tf_op | source)
XLA Modules:
  0.0 165.8 jit_solution(8107914245681863650)
XLA Ops:
  7.2 0.0 reduce-scatter.2.cloned.1.call-start
  7.2 6.4 %copy.7 = bf16[1,1,1024,2048]{2,3,1,0:T(8,128)(2,1)} copy(bf16[1,1,1024,2048]{3,2,1,0:T(8,128)(2,1)} %param.3) | data formatting | bytes 8388608 | tf_op args[0]
  13.6 0.0 reduce-scatter.2.cloned.1.call-update
  13.6 0.0 all-gather.2.cloned.1.call-start
  13.7 1.9 %copy.6 = f32[1,1024,512]{1,2,0:T(8,128)S(1)} copy(f32[1,1024,512]{2,1,0:T(8,128)} %param.4) | data formatting | bytes 4194304 | tf_op args[1]
  15.6 2.9 %copy.10 = f32[1024,512]{0,1:T(8,128)} copy(f32[1024,512]{1,0:T(8,128)} %param.5) | data formatting | bytes 4194304 | tf_op args[2]
  18.5 42.6 %reduce-scatter.2.cloned.1.call-done = bf16[1024,512]{0,1:T(8,128)(2,1)} async-done(((bf16[1024,2048]{0,1:T(8,128)(2,1)}), bf16[1024,512]{0,1:T(8,128)(2,1)}) %reduce-scatter.2.cloned.1.call-update) | async-done | bytes 1048592 | tf_op jit(solution)/shard_map/reduce_scatter | solution.py:34
  61.1 1.5 fusion.3
  62.6 0.5 copy.16
  63.1 1.8 %fusion.13 = f32[8,4,128,16]{3,0,2,1:T(8,128)S(1)} fusion(f32[8,128,4,128]{1,0,3,2:T(8,128)S(1)} %bitcast.56, f32[128]{0:T(128)S(1)} %add_multiply_fusion, f32[16]{0:T(128)S(1)} %compare_select_fusion), kind=kOutput, calls=%fused_computation.18 | convolution fusion | flops 100669440 | bytes 2359872 | tf_op jit(solution)/shard_map/kr,arbc,lc->abkl/dot_general | solution.py:24
  65.0 3.4 %fusion.1 = f32[8,4,16,16]{3,2,1,0:T(8,128)S(1)} fusion(f32[8,4,128,16]{3,0,2,1:T(8,128)S(1)} %fusion.13, f32[128]{0:T(128)S(1)} %add_multiply_fusion, f32[16]{0:T(128)S(1)} %compare_select_fusion), kind=kOutput, calls=%fused_computation.4 | convolution fusion | flops 12589056 | bytes 295488 | tf_op jit(solution)/shard_map/kr,arbc,lc->abkl/dot_general | solution.py:24
  68.4 40.2 %psum.7 = f32[8,4,16,16]{3,2,1,0:T(8,128)S(1)} all-reduce(f32[8,4,16,16]{3,2,1,0:T(8,128)S(1)} %fusion.1), channel_id=1, replica_groups=mesh['rep'=8,'fsdp'=4] {'rep'}, use_global_device_ids=true, to_apply=%region_1.2 | all-reduce | flops 8192 | bytes 65536 | tf_op jit(solution)/shard_map/psum | solution.py:43
  108.6 0.6 fusion.4
  109.2 4.8 %multiply_bitcast_fusion = f32[8,128,4,128]{3,1,2,0:T(8,128)} fusion(f32[8,4,16,128]{3,2,1,0:T(8,128)S(1)} %fusion.4, f32[128]{0:T(128)S(1)} %add_multiply_fusion, f32[16]{0:T(128)S(1)} %compare_select_fusion), kind=kOutput, calls=%fused_computation.6 | convolution fusion | flops 101193728 | bytes 2359872 | tf_op jit(solution)/shard_map/kr,abkl,lc->arbc/dot_general | solution.py:29
  114.0 2.9 %copy.9 = f32[8,128,4,128]{1,0,3,2:T(8,128)} copy(f32[8,128,4,128]{3,1,2,0:T(8,128)} %multiply_bitcast_fusion) | data formatting | bytes 4194304 | tf_op jit(solution)/shard_map/mul | solution.py:44
  116.9 4.7 %fusion.40 = (bf16[1024,512]{0,1:T(8,128)(2,1)}, f32[1024,512]{0,1:T(8,128)}) fusion(f32[1024,512]{0,1:T(8,128)} %copy.10, f32[64,8,8,128]{3,2,1,0:T(8,128)} %bitcast.54), kind=kLoop, calls=%fused_computation.48 | loop fusion | flops 1048576 | bytes 7340032 | tf_op jit(solution)/shard_map/convert_element_type | solution.py:45
  121.6 0.0 all-gather.2.cloned.1.call-update
  121.6 0.6 fusion.10
  122.2 4.8 %convolution_bitcast_fusion = f32[8,128,4,128]{3,1,2,0:T(8,128)} fusion(f32[8,4,16,128]{3,2,1,0:T(8,128)S(1)} %fusion.10, f32[128]{0:T(128)S(1)} %add_multiply_fusion, f32[16]{0:T(128)S(1)} %compare_select_fusion), kind=kOutput, calls=%fused_computation.7 | convolution fusion | flops 100669440 | bytes 2359872 | tf_op jit(solution)/shard_map/kr,abkl,lc->arbc/dot_general | solution.py:29
  127.0 0.0 copy-start.1
  127.0 3.1 %copy.8 = f32[8,128,4,128]{1,0,3,2:T(8,128)} copy(f32[8,128,4,128]{3,1,2,0:T(8,128)} %convolution_bitcast_fusion) | data formatting | bytes 4194304 | tf_op jit(solution)/shard_map/kr,abkl,lc->arbc/transpose | solution.py:29
  130.1 0.0 copy-done.1
  130.1 3.8 %fusion = f32[1,1024,512]{1,2,0:T(8,128)} fusion(f32[64,8,8,128]{3,2,1,0:T(8,128)} %bitcast.55, bf16[1024,512]{0,1:T(8,128)(2,1)S(1)} %copy-done.1, f32[1,1024,512]{1,2,0:T(8,128)S(1)} %copy.6), kind=kLoop, calls=%fused_computation.2 | loop fusion | flops 2097152 | bytes 7340032 | tf_op jit(solution)/shard_map/broadcast_in_dim | solution.py:46
  133.8 0.0 copy-start
  133.8 3.0 %copy.11 = f32[1,1024,512]{2,1,0:T(8,128)} copy(f32[1,1024,512]{1,2,0:T(8,128)} %fusion) | data formatting | bytes 4194304
  136.9 0.0 copy-done
  136.9 1.8 %copy.12 = f32[1024,512]{1,0:T(8,128)} copy(f32[1024,512]{0,1:T(8,128)S(1)} %copy-done) | data formatting | bytes 4194304
  138.7 13.9 %all-gather.2.cloned.1.call-done = bf16[1024,2048]{0,1:T(8,128)(2,1)} async-done(((bf16[1024,512]{0,1:T(8,128)(2,1)}), bf16[1024,2048]{0,1:T(8,128)(2,1)}) %all-gather.2.cloned.1.call-update) | async-done | bytes 4194320 | tf_op jit(solution)/shard_map/all_gather | solution.py:45
  152.6 6.4 %copy.13 = bf16[1024,2048]{1,0:T(8,128)(2,1)} copy(bf16[1024,2048]{0,1:T(8,128)(2,1)} %all-gather.2.cloned.1.call-done) | data formatting | bytes 8388608
  (2 shorter events, 0.0 us)
Async XLA Ops:
  7.2 53.9 %reduce-scatter.2.cloned.1.call-start = ((), (), s32[]{:S(2)}) async-start(), calls=%async_computation.1 | async-start | bytes 5242880 | tf_op jit(solution)/shard_map/reduce_scatter | solution.py:34
  13.6 139.0 %all-gather.2.cloned.1.call-start = ((), (), s32[]{:S(2)}) async-start(), calls=%async_computation.2 | async-start | bytes 5242880 | tf_op jit(solution)/shard_map/all_gather | solution.py:45
  127.0 3.1 %copy-start.1 = (bf16[1024,512]{0,1:T(8,128)(2,1)S(1)}, bf16[1024,512]{0,1:T(8,128)(2,1)}, u32[]{:S(2)}) copy-start(bf16[1024,512]{0,1:T(8,128)(2,1)} %reduce-scatter.2.cloned.1.call-done) | copy-start | bytes 3145732
  133.8 3.0 %copy-start = (f32[1024,512]{0,1:T(8,128)S(1)}, f32[1024,512]{0,1:T(8,128)}, u32[]{:S(2)}) copy-start(f32[1024,512]{0,1:T(8,128)} %get-tuple-element.7) | copy-start | bytes 6291460
Sparse Core Ops, SparseCore 0:
  13.8 47.2 reduce-scatter.1
  121.7 30.8 all-gather.1
where the time goes:
time: 166 us
  waiting for transfers between devices  56.5 us (34%)
  blocking collectives  40.2 us (24%)
  local copies, waits for them, and re-layouts  28.9 us (17%)
  matrix products  16 us (10%)
  between operations  14.1 us (8%)
  other arithmetic  10 us (6%)
    reduce_scatter x1, waiting for transfers between devices, local(): lax.psum_scatter(gradients[0, 0].astype(jnp.float32).astype(jnp.bfloat16)...  42.6 us
    psum x1, blocking collectives, local(): mean_band = lax.psum(own_band, 'rep') / lax.axis_size('rep')  40.2 us
    unnamed x11, local copies, waits for them, and re-layouts  22.9 us
    all_gather x1, waiting for transfers between devices, local(): lax.all_gather(new_master.astype(jnp.bfloat16), 'fsdp', axis=1, tiled=True)  13.9 us
    dot_general x4, matrix products, spread_band(): jnp.einsum('kr,abkl,lc->arbc', table, coeffs, table, precision=lax.Precis...  10.8 us
    dot_general x2, matrix products, band_of(): jnp.einsum('kr,arbc,lc->abkl', table, blocks, table, precision=lax.Precis...  5.25 us
    convert_element_type x1, other arithmetic, local(): new_master.astype(jnp.bfloat16)  4.72 us
    broadcast_in_dim x1, other arithmetic, local(): return (remaining[None], new_master, weights_full)  3.75 us
  transfers between devices with their start and end apart: 2, of which 2 were waited for; matrix products, arithmetic and copies ran while one was open for 13% of the time, Pallas kernels for 0%

commit v1 on v0

--- a/solution.py
+++ b/solution.py
@@ -7,6 +7,12 @@
 BAND = 16
 momentum_decay = 0.9
 step_size = 0.05
+
+
+def add_all(x, axis):
+    parts = lax.all_gather(x, axis, axis=0, tiled=False)
+    summed = parts.sum(axis=0)
+    return summed
 
 
 def cosine_rows():
@@ -40,7 +46,7 @@
     moment = momentum_decay * momentum[0] + summed
     own_band = band_of(moment)
     remaining = moment - spread_band(own_band)
-    mean_band = lax.psum(own_band, "rep") / lax.axis_size("rep")
+    mean_band = add_all(own_band, "rep") / lax.axis_size("rep")
     new_master = master_weights - step_size * spread_band(mean_band)
     weights_full = lax.all_gather(new_master.astype(jnp.bfloat16), "fsdp", axis=1, tiled=True)
     return (remaining[None], new_master, weights_full)

time: 166 us -> 176 us (1.060)
  blocking collectives: 40.2 us -> 44.9 us
  waiting for transfers between devices: 56.5 us -> 59.2 us
  other arithmetic: 10 us -> 12 us
    all_gather x0 -> x1, blocking collectives: none -> 44.9 us  [add_all(): parts = lax.all_gather(x, axis, axis=0, tiled=False)]
    psum x1 -> x0, blocking collectives: 40.2 us -> none  [local(): mean_band = lax.psum(own_band, 'rep') / lax.axis_size('rep')]
    all_gather x1, waiting for transfers between devices: 13.9 us -> 16.6 us  [local(): lax.all_gather(new_master.astype(jnp.bfloat16), 'fsdp', axis=1, tiled=True)]
    reduce_sum x0 -> x1, other arithmetic: none -> 1.83 us  [add_all(): summed = parts.sum(axis=0)]
where the time goes in v1:
time: 176 us; the launch traced here: 175 us
  waiting for transfers between devices  59.2 us (34%)
  blocking collectives  44.9 us (26%)
  local copies, waits for them, and re-layouts  29 us (16%)
  matrix products  16 us (9%)
  between operations  14.1 us (8%)
  other arithmetic  12 us (7%)
    all_gather x1, blocking collectives, add_all(): parts = lax.all_gather(x, axis, axis=0, tiled=False)  44.9 us
    reduce_scatter x1, waiting for transfers between devices, local(): lax.psum_scatter(gradients[0, 0].astype(jnp.float32).astype(jnp.bfloat16)...  42.6 us
    unnamed x11, local copies, waits for them, and re-layouts  22.9 us
    all_gather x1, waiting for transfers between devices, local(): lax.all_gather(new_master.astype(jnp.bfloat16), 'fsdp', axis=1, tiled=True)  16.6 us
    dot_general x4, matrix products, spread_band(): jnp.einsum('kr,abkl,lc->arbc', table, coeffs, table, precision=lax.Precis...  10.8 us
    dot_general x2, matrix products, band_of(): jnp.einsum('kr,arbc,lc->abkl', table, blocks, table, precision=lax.Precis...  5.25 us
    convert_element_type x1, other arithmetic, local(): new_master.astype(jnp.bfloat16)  4.72 us
    broadcast_in_dim x1, other arithmetic, local(): return (remaining[None], new_master, weights_full)  3.84 us
  transfers between devices with their start and end apart: 2, of which 2 were waited for; matrix products, arithmetic and copies ran while one was open for 13% of the time, Pallas kernels for 0%

profile of v1, /device:TPU:0, one launch (start us, length us, event | category | flops | bytes accessed | tf_op | source)
XLA Modules:
  0.0 175.2 jit_solution(8242003757176742835)
XLA Ops:
  7.2 0.0 reduce-scatter.2.cloned.1.call-start
  7.2 6.4 %copy.25 = bf16[1,1,1024,2048]{2,3,1,0:T(8,128)(2,1)} copy(bf16[1,1,1024,2048]{3,2,1,0:T(8,128)(2,1)} %param.3) | data formatting | bytes 8388608 | tf_op args[0]
  13.6 0.0 reduce-scatter.2.cloned.1.call-update
  13.6 0.0 all-gather.3.cloned.1.call-start
  13.7 1.9 %copy.24 = f32[1,1024,512]{1,2,0:T(8,128)S(1)} copy(f32[1,1024,512]{2,1,0:T(8,128)} %param.4) | data formatting | bytes 4194304 | tf_op args[1]
  15.6 2.9 %copy.31 = f32[1024,512]{0,1:T(8,128)} copy(f32[1024,512]{1,0:T(8,128)} %param.5) | data formatting | bytes 4194304 | tf_op args[2]
  18.5 42.6 %reduce-scatter.2.cloned.1.call-done = bf16[1024,512]{0,1:T(8,128)(2,1)} async-done(((bf16[1024,2048]{0,1:T(8,128)(2,1)}), bf16[1024,512]{0,1:T(8,128)(2,1)}) %reduce-scatter.2.cloned.1.call-update) | async-done | bytes 1048592 | tf_op jit(solution)/shard_map/reduce_scatter | solution.py:40
  61.1 1.5 fusion.3
  62.6 0.5 copy.38
  63.1 1.8 %fusion.13 = f32[8,4,128,16]{3,0,2,1:T(8,128)S(1)} fusion(f32[8,128,4,128]{1,0,3,2:T(8,128)S(1)} %bitcast.58, f32[128]{0:T(128)S(1)} %add_multiply_fusion, f32[16]{0:T(128)S(1)} %compare_select_fusion), kind=kOutput, calls=%fused_computation.18 | convolution fusion | flops 100669440 | bytes 2359872 | tf_op jit(solution)/shard_map/kr,arbc,lc->abkl/dot_general | solution.py:30
  65.0 3.4 %fusion.1 = f32[8,4,16,16]{3,2,1,0:T(8,128)S(1)} fusion(f32[8,4,128,16]{3,0,2,1:T(8,128)S(1)} %fusion.13, f32[128]{0:T(128)S(1)} %add_multiply_fusion, f32[16]{0:T(128)S(1)} %compare_select_fusion), kind=kOutput, calls=%fused_computation.4 | convolution fusion | flops 12589056 | bytes 295488 | tf_op jit(solution)/shard_map/kr,arbc,lc->abkl/dot_general | solution.py:30
  68.4 44.9 %all-gather = f32[64,4,16,16]{3,2,1,0:T(8,128)} all-gather(f32[8,4,16,16]{3,2,1,0:T(8,128)S(1)} %fusion.1), channel_id=2, replica_groups=mesh['rep'=8,'fsdp'=4] {'rep'}, dimensions={0}, use_global_device_ids=true | all-gather | bytes 294912 | tf_op jit(solution)/shard_map/all_gather | solution.py:13
  113.3 1.8 %reduce_sum.9 = f32[8,4,16,16]{3,2,1,0:T(8,128)S(1)} reduce(f32[8,8,4,16,16]{4,3,2,1,0:T(8,128)} %bitcast.57, f32[]{:T(128)} %constant.10.clone.1), dimensions={0}, to_apply=%region_1.2 | reduce | flops 57344 | bytes 294916 | tf_op jit(solution)/shard_map/reduce_sum | solution.py:14
  115.1 0.6 fusion.4
  115.7 4.8 %multiply_bitcast_fusion = f32[8,128,4,128]{3,1,2,0:T(8,128)} fusion(f32[8,4,16,128]{3,2,1,0:T(8,128)S(1)} %fusion.4, f32[128]{0:T(128)S(1)} %add_multiply_fusion, f32[16]{0:T(128)S(1)} %compare_select_fusion), kind=kOutput, calls=%fused_computation.6 | convolution fusion | flops 101193728 | bytes 2359872 | tf_op jit(solution)/shard_map/kr,abkl,lc->arbc/dot_general | solution.py:35
  120.5 2.9 %copy.30 = f32[8,128,4,128]{1,0,3,2:T(8,128)} copy(f32[8,128,4,128]{3,1,2,0:T(8,128)} %multiply_bitcast_fusion) | data formatting | bytes 4194304 | tf_op jit(solution)/shard_map/mul | solution.py:50
  123.4 4.7 %fusion.40 = (bf16[1024,512]{0,1:T(8,128)(2,1)}, f32[1024,512]{0,1:T(8,128)}) fusion(f32[1024,512]{0,1:T(8,128)} %copy.31, f32[64,8,8,128]{3,2,1,0:T(8,128)} %bitcast.55), kind=kLoop, calls=%fused_computation.48 | loop fusion | flops 1048576 | bytes 7340032 | tf_op jit(solution)/shard_map/convert_element_type | solution.py:51
  128.1 0.0 all-gather.3.cloned.1.call-update
  128.1 0.6 fusion.10
  128.7 4.8 %convolution_bitcast_fusion = f32[8,128,4,128]{3,1,2,0:T(8,128)} fusion(f32[8,4,16,128]{3,2,1,0:T(8,128)S(1)} %fusion.10, f32[128]{0:T(128)S(1)} %add_multiply_fusion, f32[16]{0:T(128)S(1)} %compare_select_fusion), kind=kOutput, calls=%fused_computation.7 | convolution fusion | flops 100669440 | bytes 2359872 | tf_op jit(solution)/shard_map/kr,abkl,lc->arbc/dot_general | solution.py:35
  133.5 0.0 copy-start.1
  133.5 3.2 %copy.28 = f32[8,128,4,128]{1,0,3,2:T(8,128)} copy(f32[8,128,4,128]{3,1,2,0:T(8,128)} %convolution_bitcast_fusion) | data formatting | bytes 4194304 | tf_op jit(solution)/shard_map/kr,abkl,lc->arbc/transpose | solution.py:35
  136.7 0.0 copy-done.1
  136.7 3.8 %fusion = f32[1,1024,512]{1,2,0:T(8,128)} fusion(f32[64,8,8,128]{3,2,1,0:T(8,128)} %bitcast.56, bf16[1024,512]{0,1:T(8,128)(2,1)S(1)} %copy-done.1, f32[1,1024,512]{1,2,0:T(8,128)S(1)} %copy.24), kind=kLoop, calls=%fused_computation.2 | loop fusion | flops 2097152 | bytes 7340032 | tf_op jit(solution)/shard_map/broadcast_in_dim | solution.py:52
  140.5 0.0 copy-start
  140.5 3.0 %copy.32 = f32[1,1024,512]{2,1,0:T(8,128)} copy(f32[1,1024,512]{1,2,0:T(8,128)} %fusion) | data formatting | bytes 4194304
  143.6 0.0 copy-done
  143.6 1.8 %copy.33 = f32[1024,512]{1,0:T(8,128)} copy(f32[1024,512]{0,1:T(8,128)S(1)} %copy-done) | data formatting | bytes 4194304
  145.4 16.6 %all-gather.3.cloned.1.call-done = bf16[1024,2048]{0,1:T(8,128)(2,1)} async-done(((bf16[1024,512]{0,1:T(8,128)(2,1)}), bf16[1024,2048]{0,1:T(8,128)(2,1)}) %all-gather.3.cloned.1.call-update) | async-done | bytes 4194320 | tf_op jit(solution)/shard_map/all_gather | solution.py:51
  161.9 6.4 %copy.34 = bf16[1024,2048]{1,0:T(8,128)(2,1)} copy(bf16[1024,2048]{0,1:T(8,128)(2,1)} %all-gather.3.cloned.1.call-done) | data formatting | bytes 8388608
  (2 shorter events, 0.0 us)
Async XLA Ops:
  7.2 53.9 %reduce-scatter.2.cloned.1.call-start = ((), (), s32[]{:S(2)}) async-start(), calls=%async_computation.1 | async-start | bytes 5242880 | tf_op jit(solution)/shard_map/reduce_scatter | solution.py:40
  13.6 148.3 %all-gather.3.cloned.1.call-start = ((), (), s32[]{:S(2)}) async-start(), calls=%async_computation.2 | async-start | bytes 5242880 | tf_op jit(solution)/shard_map/all_gather | solution.py:51
  133.5 3.2 %copy-start.1 = (bf16[1024,512]{0,1:T(8,128)(2,1)S(1)}, bf16[1024,512]{0,1:T(8,128)(2,1)}, u32[]{:S(2)}) copy-start(bf16[1024,512]{0,1:T(8,128)(2,1)} %reduce-scatter.2.cloned.1.call-done) | copy-start | bytes 3145732
  140.5 3.0 %copy-start = (f32[1024,512]{0,1:T(8,128)S(1)}, f32[1024,512]{0,1:T(8,128)}, u32[]{:S(2)}) copy-start(f32[1024,512]{0,1:T(8,128)} %get-tuple-element.13) | copy-start | bytes 6291460
Sparse Core Ops, SparseCore 0:
  13.8 47.2 reduce-scatter.1
  128.2 33.6 all-gather.2
